TPU v7x, 128 devices: a whole 4x4x4 slice. The times are simulated.
128 devices in a mesh: row: 32 (over z, y, core), col: 4 (over x).
Axes of the slice: x: 4, y: 4, z: 4, core: 2. Of those that a mesh axis runs over, the one named last changes fastest.
Arguments:
- matrix: float32 [1, 32, 512, 8, 4, 512], P(None, 'row', None, None, 'col'), may hold values from -30 to 30, as said below
Outputs:
- factored: float32 [1, 32, 512, 8, 4, 512], P(None, 'row', None, None, 'col')
Inputs may be any that keep to these rules, and one draw needn't show every extreme that they name: matrix is symmetric, positive definite and well conditioned.
All inputs are finite; a program needn't handle non-finite values.
Results may differ from a plain program's by a relative error of at most 0.00013.
Values sent between devices are 32-bit elements; how exact they have to be, the bound alone decides.
A program may use at most 192 MiB of HBM per device.

v0:
```python
import jax
import jax.numpy as jnp
from jax import lax
from jax.sharding import PartitionSpec as P

NB = 512
STEPS = 2


def spread(value, axis, source):
    kept = jnp.where(lax.axis_index(axis) == source, value, 0).astype(value.dtype)
    return lax.psum(kept, axis)


def from_root(shard, axis, root):
    return lax.dynamic_index_in_dim(lax.all_gather(shard, axis), root, 0, keepdims=False)


def trailing_product(column_panel, transposed):
    return jnp.einsum(
        "tan,sbn->tasb",
        column_panel,
        transposed,
        precision=lax.Precision.HIGHEST,
        preferred_element_type=jnp.float32,
    )


def shards(matrix):
    local_rows = matrix.shape[0]
    local_cols = matrix.shape[3]
    blocks = matrix.reshape(local_rows, NB, local_cols, NB)
    row_count = lax.axis_size("row")
    column_count = lax.axis_size("col")
    group_size = row_count // column_count
    row_place = lax.axis_index("row")
    column_place = lax.axis_index("col")
    tile_rows = jnp.arange(local_rows, dtype=jnp.int32) * row_count + row_place
    tile_columns = jnp.arange(local_cols, dtype=jnp.int32) * column_count + column_place
    anchor = jnp.int32(0)

    def fetch_columns(column_panel):
        empty = jnp.zeros((local_rows, group_size, NB, NB), jnp.float32)
        slot_index = row_place // column_count
        holder = row_place % column_count == column_place
        contribution = jnp.where(holder, column_panel, 0.0)
        filled = lax.dynamic_update_slice(
            empty, contribution[:, None], (anchor, slot_index, anchor, anchor)
        )
        gathered = lax.psum(filled, "row")
        return gathered.reshape(local_cols, NB, NB)

    def factor_step(blocks, step):
        root_row = step % row_count
        local_row = step // row_count
        root_col = step % column_count
        local_col = step // column_count
        corner = blocks[local_row, :, local_col, :]
        owner = (row_place == root_row) & (column_place == root_col)
        identity = jnp.eye(NB, dtype=jnp.float32)
        chosen = jnp.where(owner, corner, identity)
        factor_local = jnp.linalg.cholesky(chosen)
        diag_block = spread(factor_local, "row", root_row)
        source = blocks[:, :, local_col, :]
        solved = jax.scipy.linalg.solve_triangular(
            diag_block, source.reshape(local_rows * NB, NB).T, lower=True
        ).T
        solved = solved.reshape(local_rows, NB, NB)
        panel_local = jnp.where((tile_rows > step)[:, None, None], solved, 0.0)
        column_panel = from_root(panel_local, "col", root_col)
        transposed = fetch_columns(column_panel)
        return (diag_block, column_panel, transposed)

    factors = factor_step(blocks, 0)
    for step in range(STEPS):
        diag_block, column_panel, transposed = factors
        write_blocks = blocks
        write_local_row = step // row_count
        write_local_col = step // column_count
        column_now = write_blocks[:, :, write_local_col, :]
        owns_col = column_place == step % column_count
        row_after = (tile_rows > step)[:, None, None]
        row_hit = (tile_rows == step)[:, None, None]
        new_column = jnp.where(
            row_after, column_panel, jnp.where(row_hit, diag_block[None], column_now)
        )
        new_column = jnp.where(owns_col, new_column, column_now)
        write_blocks = write_blocks.at[:, :, write_local_col, :].set(new_column)
        row_now = write_blocks[write_local_row]
        owns_row = row_place == step % row_count
        zero_cols = (tile_columns > step)[None, :, None]
        new_row = jnp.where(owns_row & zero_cols, 0.0, row_now)
        blocks = write_blocks.at[write_local_row].set(new_row)
        if step + 1 < STEPS:
            next_col = (step + 1) // column_count
            single = trailing_product(column_panel, transposed[next_col : next_col + 1])
            blocks = blocks.at[:, :, next_col, :].set(
                blocks[:, :, next_col, :] - single[:, :, 0, :]
            )
            factors = factor_step(blocks, step + 1)
            rest = transposed.at[next_col].set(jnp.zeros((NB, NB), jnp.float32))
            blocks = blocks - trailing_product(column_panel, rest)
        else:
            blocks = blocks - trailing_product(column_panel, transposed)
    return blocks.reshape(matrix.shape)


def solution(mesh):
    in_specs = (P(None, "row", None, None, "col", None),)
    out_specs = P(None, "row", None, None, "col", None)
    return jax.shard_map(shards, mesh=mesh, in_specs=in_specs, out_specs=out_specs, check_vma=False)
```

profile of v0, /device:TPU:1, one launch (start us, length us, event | category | flops | bytes accessed | tf_op | source)
XLA Modules:
  0.0 936.6 jit_solution(8377719153286255205)
XLA Ops:
  6.5 20.5 %copy.2 = f32[1,1,512,8,1,512]{2,5,3,4,1,0:T(8,128)} copy(f32[1,1,512,8,1,512]{5,4,3,2,1,0:T(1,128)} %param.16) | data formatting | bytes 16777216 | tf_op args[0]
  27.1 1.3 convert_select_fusion.1
  28.8 1.5 fusion.5
  30.2 11.7 %cholesky.286 = f32[128,128]{1,0:T(8,128)S(1)} custom-call(f32[128,128]{1,0:T(8,128)S(1)} %cholesky.426), custom_call_target="Cholesky" | custom-call | tf_op jit(solution)/shard_map/jit(cholesky)/cholesky | solution.py:62
  42.1 9.8 %custom-call.27 = f32[1,128,128]{1,2,0:T(8,128)S(1)} custom-call(f32[1,128,128]{2,1,0:T(8,128)S(1)} %get-tuple-element.136), custom_call_target="InvertDiagBlocksLowerTriangular" | custom-call | tf_op jit(solution)/shard_map/jit(cholesky)/cholesky | solution.py:62
  52.7 11.7 %cholesky.305 = f32[128,128]{1,0:T(8,128)S(1)} custom-call(f32[128,128]{1,0:T(8,128)S(1)} %cholesky.430), custom_call_target="Cholesky" | custom-call | tf_op jit(solution)/shard_map/jit(cholesky)/cholesky | solution.py:62
  64.6 10.2 %custom-call.28 = f32[1,128,128]{1,2,0:T(8,128)S(1)} custom-call(f32[1,128,128]{2,1,0:T(8,128)S(1)} %get-tuple-element.134), custom_call_target="InvertDiagBlocksLowerTriangular" | custom-call | tf_op jit(solution)/shard_map/jit(cholesky)/cholesky | solution.py:62
  75.9 11.7 %cholesky.326 = f32[128,128]{1,0:T(8,128)S(1)} custom-call(f32[128,128]{1,0:T(8,128)S(1)} %cholesky.435), custom_call_target="Cholesky" | custom-call | tf_op jit(solution)/shard_map/jit(cholesky)/cholesky | solution.py:62
  87.8 9.8 %custom-call.29 = f32[1,128,128]{1,2,0:T(8,128)S(1)} custom-call(f32[1,128,128]{2,1,0:T(8,128)S(1)} %get-tuple-element.132), custom_call_target="InvertDiagBlocksLowerTriangular" | custom-call | tf_op jit(solution)/shard_map/jit(cholesky)/cholesky | solution.py:62
  98.4 11.9 %cholesky.343 = f32[128,128]{1,0:T(8,128)S(1)} custom-call(f32[128,128]{1,0:T(8,128)S(1)} %convolution_subtract_fusion.12), custom_call_target="Cholesky" | custom-call | tf_op jit(solution)/shard_map/jit(cholesky)/cholesky | solution.py:62
  115.0 1.1 fusion.10
  116.2 1.5 slice_bitcast_fusion.20
  117.7 107.4 %all-reduce.6.cloned.1.call-done = f32[512,512]{0,1:T(8,128)} async-done(((f32[512,512]{0,1:T(8,128)}), f32[512,512]{0,1:T(8,128)}) %all-reduce.6.cloned.1.call-update) | async-done | bytes 1048592 | tf_op jit(solution)/shard_map/psum | solution.py:12
  225.1 1.3 fusion.9
  226.5 8.2 while.10
  227.2 1.3 dynamic-slice.63
  229.2 1.3 dynamic-slice.63
  231.3 1.3 dynamic-slice.63
  233.3 1.3 dynamic-slice.63
  235.4 40.1 %custom-call.30 = f32[4,128,128]{1,2,0:T(8,128)S(1)} custom-call(f32[4,128,128]{2,1,0:T(8,128)} %copy-done.4), custom_call_target="InvertDiagBlocksLowerTriangular" | custom-call | tf_op jit(solution)/shard_map/jit(_solve_triangular)/triangular_solve | solution.py:65
  278.9 1.1 fusion
  280.1 47.6 %all-gather.5.cloned.1.call-done = f32[2048,512]{0,1:T(8,128)} async-done(((f32[512,512]{0,1:T(8,128)}), f32[2048,512]{0,1:T(8,128)}) %all-gather.5.cloned.1.call-update) | async-done | bytes 4194320 | tf_op jit(solution)/shard_map/all_gather | solution.py:16
  327.7 1.3 select_bitcast_fusion.1
  329.3 4.3 broadcast.342
  333.6 1.1 constant_dynamic-update-slice_fusion.3
  335.1 2.6 bitcast_dynamic-update-slice_fusion.4
  337.7 8.5 broadcast_select_fusion
  346.1 109.5 %all-reduce.8.cloned.1.call-done = f32[1,8,512,512]{3,2,1,0:T(8,128)} async-done(((f32[1,8,512,512]{3,2,1,0:T(8,128)}), f32[1,8,512,512]{3,2,1,0:T(8,128)}) %all-reduce.8.cloned.1.call-update) | async-done | bytes 8388624 | tf_op jit(solution)/shard_map/psum | solution.py:50
  455.6 3.7 convert_select_fusion
  461.0 11.7 %cholesky.358 = f32[128,128]{1,0:T(8,128)S(1)} custom-call(f32[128,128]{1,0:T(8,128)S(1)} %cholesky.439), custom_call_target="Cholesky" | custom-call | tf_op jit(solution)/shard_map/jit(cholesky)/cholesky | solution.py:62
  472.9 9.8 %custom-call.31 = f32[1,128,128]{1,2,0:T(8,128)S(1)} custom-call(f32[1,128,128]{2,1,0:T(8,128)S(1)} %get-tuple-element.130), custom_call_target="InvertDiagBlocksLowerTriangular" | custom-call | tf_op jit(solution)/shard_map/jit(cholesky)/cholesky | solution.py:62
  482.7 1.2 fusion.37
  484.1 1.3 convolution_subtract_fusion.7
  485.4 12.1 %cholesky.377 = f32[128,128]{1,0:T(8,128)S(1)} custom-call(f32[128,128]{1,0:T(8,128)S(1)} %cholesky.443), custom_call_target="Cholesky" | custom-call | tf_op jit(solution)/shard_map/jit(cholesky)/cholesky | solution.py:62
  497.6 9.8 %custom-call.32 = f32[1,128,128]{1,2,0:T(8,128)S(1)} custom-call(f32[1,128,128]{2,1,0:T(8,128)S(1)} %get-tuple-element.128), custom_call_target="InvertDiagBlocksLowerTriangular" | custom-call | tf_op jit(solution)/shard_map/jit(cholesky)/cholesky | solution.py:62
  507.9 1.5 convolution_subtract_fusion.9
  509.4 11.7 %cholesky.398 = f32[128,128]{1,0:T(8,128)S(1)} custom-call(f32[128,128]{1,0:T(8,128)S(1)} %cholesky.448), custom_call_target="Cholesky" | custom-call | tf_op jit(solution)/shard_map/jit(cholesky)/cholesky | solution.py:62
  521.3 9.8 %custom-call.33 = f32[1,128,128]{1,2,0:T(8,128)S(1)} custom-call(f32[1,128,128]{2,1,0:T(8,128)S(1)} %get-tuple-element.126), custom_call_target="InvertDiagBlocksLowerTriangular" | custom-call | tf_op jit(solution)/shard_map/jit(cholesky)/cholesky | solution.py:62
  531.4 1.5 convolution_subtract_fusion.11
  532.9 11.7 %cholesky.415 = f32[128,128]{1,0:T(8,128)S(1)} custom-call(f32[128,128]{1,0:T(8,128)S(1)} %convolution_subtract_fusion.11), custom_call_target="Cholesky" | custom-call | tf_op jit(solution)/shard_map/jit(cholesky)/cholesky | solution.py:62
  550.1 1.2 select_select_fusion
  551.4 105.4 %all-reduce.10.cloned.1.call-done = f32[512,512]{0,1:T(8,128)} async-done(((f32[512,512]{0,1:T(8,128)}), f32[512,512]{0,1:T(8,128)}) %all-reduce.10.cloned.1.call-update) | async-done | bytes 1048592 | tf_op jit(solution)/shard_map/psum | solution.py:12
  656.7 1.3 fusion.7
  658.1 8.7 while.11
  658.8 1.4 dynamic-slice.65
  660.9 1.4 dynamic-slice.65
  663.1 1.4 dynamic-slice.65
  665.3 1.4 dynamic-slice.65
  666.8 39.3 %custom-call.34 = f32[4,128,128]{1,2,0:T(8,128)S(1)} custom-call(f32[4,128,128]{2,1,0:T(8,128)S(1)} %get-tuple-element.94), custom_call_target="InvertDiagBlocksLowerTriangular" | custom-call | tf_op jit(solution)/shard_map/jit(_solve_triangular)/triangular_solve | solution.py:65
  709.4 1.4 fusion.49
  710.8 1.1 fusion.1
  712.2 47.4 %all-gather.7.cloned.1.call-done = f32[2048,512]{1,0:T(8,128)} async-done(((f32[512,512]{1,0:T(8,128)}), f32[2048,512]{1,0:T(8,128)}) %all-gather.7.cloned.1.call-update) | async-done | bytes 4194320 | tf_op jit(solution)/shard_map/all_gather | solution.py:16
  759.6 1.3 slice.267
  761.3 1.2 select_bitcast_fusion
  762.4 1.6 copy.32
  764.0 4.3 broadcast.351
  768.3 1.1 constant_dynamic-update-slice_fusion.2
  769.4 1.1 broadcast_dynamic-update-slice_fusion
  771.6 16.7 %bitcast_subtract_fusion = f32[1,512,8,512]{1,3,2,0:T(8,128)S(1)} fusion(f32[1,512,8,512]{1,3,2,0:T(8,128)} %bitcast_dynamic-update-slice_fusion.3, f32[8,512,512]{2,1,0:T(8,128)} %broadcast_dynamic-update-slice_fusion, f32[2048,512]{0,1:T(8,128)} %all-gather.5.cloned.1.call-done), kind=kOutput, calls=%fused_computation.4 | convolution fusion | flops 12886999040 | bytes 26214400 | tf_op jit(solution)/shard_map/tan,sbn->tasb/dot_general | solution.py:20
  788.3 3.4 copy.98
  791.7 1.3 bitcast_dynamic-update-slice_fusion.2
  793.0 97.3 %all-reduce.12.cloned.1.call-done = f32[8,512,512]{2,1,0:T(8,128)} async-done(((f32[8,512,512]{2,1,0:T(8,128)}), f32[8,512,512]{2,1,0:T(8,128)}) %all-reduce.12.cloned.1.call-update) | async-done | bytes 8388624 | tf_op jit(solution)/shard_map/psum | solution.py:50
  890.3 18.7 %subtract_bitcast_fusion = f32[1,1,512,8,1,512]{2,5,3,4,1,0:T(8,128)} fusion(f32[512,8,512]{0,2,1:T(8,128)} %bitcast_dynamic-update-slice_fusion.2, pred[8]{0:T(512)(128)(4,1)S(1)} %compare_and_fusion.1, f32[8,512,512]{2,1,0:T(8,128)} %all-reduce.12.cloned.1.call-done, f32[2048,512]{1,0:T(8,128)} %all-gather.7.cloned.1.call-done), kind=kOutput, calls=%fused_computation.5 | convolution fusion | flops 12889096192 | bytes 26214408 | tf_op jit(solution)/shard_map/tan,sbn->tasb/dot_general | solution.py:20
  909.0 20.5 %copy.35 = f32[1,1,512,8,1,512]{5,4,3,2,1,0:T(1,128)} copy(f32[1,1,512,8,1,512]{2,5,3,4,1,0:T(8,128)} %subtract_bitcast_fusion) | data formatting | bytes 16777216 | tf_op jit(solution)/shard_map/reshape | solution.py:105
  (131 shorter events, 27.0 us)
Async XLA Ops:
  6.5 218.6 %all-reduce.6.cloned.1.call-start = ((), (), s32[]{:S(2)}) async-start(), calls=%async_computation | async-start | bytes 2097152 | tf_op jit(solution)/shard_map/psum | solution.py:12
  116.1 211.6 %all-gather.5.cloned.1.call-start = ((), (), s32[]{:S(2)}) async-start(), calls=%async_computation.4 | async-start | bytes 5242880 | tf_op jit(solution)/shard_map/all_gather | solution.py:16
  234.7 0.7 copy-start.4
  280.0 175.6 %all-reduce.8.cloned.1.call-start = ((), (), s32[]{:S(2)}) async-start(), calls=%async_computation.1 | async-start | bytes 16777216 | tf_op jit(solution)/shard_map/psum | solution.py:50
  329.3 5.7 copy-start
  334.8 321.9 %all-reduce.10.cloned.1.call-start = ((), (), s32[]{:S(2)}) async-start(), calls=%async_computation.2 | async-start | bytes 2097152 | tf_op jit(solution)/shard_map/psum | solution.py:12
  460.0 1.1 copy-start.2
  551.3 208.3 %all-gather.7.cloned.1.call-start = ((), (), s32[]{:S(2)}) async-start(), calls=%async_computation.5 | async-start | bytes 5242880 | tf_op jit(solution)/shard_map/all_gather | solution.py:16
  706.1 1.8 copy-start.3
  712.0 178.4 %all-reduce.12.cloned.1.call-start = ((), (), s32[]{:S(2)}) async-start(), calls=%async_computation.3 | async-start | bytes 16777216 | tf_op jit(solution)/shard_map/psum | solution.py:50
  788.3 3.4 copy-start.1
Sparse Core Ops, SparseCore 0:
  116.2 108.8 all-reduce.5
  280.1 47.4 all-gather.4
  334.9 120.6 all-reduce.7
  551.4 105.2 all-reduce.9
  712.1 47.5 all-gather.6
  769.5 120.7 all-reduce.11
where the time goes:
time: 947 us; the launch traced here: 937 us
  waiting for transfers between devices  515 us (54%)
  other arithmetic  263 us (28%)
  local copies, waits for them, and re-layouts  83.2 us (9%)
  matrix products  55 us (6%)
  between operations  19.6 us (2%)
    psum x2, waiting for transfers between devices, spread(): return lax.psum(kept, axis)  213 us
    psum x2, waiting for transfers between devices, fetch_columns(): gathered = lax.psum(filled, 'row')  207 us
    another operation x29, other arithmetic, factor_step(): factor_local = jnp.linalg.cholesky(chosen)  159 us
    all_gather x2, waiting for transfers between devices, from_root(): lax.all_gather(shard, axis)  95 us
    another operation x5, other arithmetic, factor_step(): jax.scipy.linalg.solve_triangular(diag_block, source.reshape(local_rows *...  82.1 us
    dot_general x3, matrix products, trailing_product(): jnp.einsum('tan,sbn->tasb', column_panel, transposed, precision=lax.Preci...  39.1 us
    unnamed x13, local copies, waits for them, and re-layouts  26 us
    reshape x1, local copies, waits for them, and re-layouts, shards(): return blocks.reshape(matrix.shape)  20.5 us
  transfers between devices with their start and end apart: 6, of which 6 were waited for; matrix products, arithmetic and copies ran while one was open for 4% of the time, Pallas kernels for 0%

commit v1 on v0

--- a/solution.py
+++ b/solution.py
@@ -47,7 +47,11 @@
         filled = lax.dynamic_update_slice(
             empty, contribution[:, None], (anchor, slot_index, anchor, anchor)
         )
-        gathered = lax.psum(filled, "row")
+        gathered = filled
+        for hop in (1, 2, 4, 8, 16):
+            gathered = gathered + lax.ppermute(
+                gathered, "row", [(dev, dev ^ hop) for dev in range(32)]
+            )
         return gathered.reshape(local_cols, NB, NB)
 
     def factor_step(blocks, step):

time: 947 us -> 2260 us (2.39)
  waiting for transfers between devices: 515 us -> 1740 us
  other arithmetic: 263 us -> 339 us
    ppermute x0 -> x10, waiting for transfers between devices: none -> 1420 us  [fetch_columns(): lax.ppermute(gathered, 'row', [(dev, dev ^ hop) for dev in range(32)])]
    psum x2 -> x0, waiting for transfers between devices: 207 us -> none  [fetch_columns(): gathered = lax.psum(filled, 'row')]
    add x0 -> x9, other arithmetic: none -> 78.1 us  [fetch_columns(): gathered + lax.ppermute(gathered, 'row', [(dev, dev ^ hop) for dev in ran...]
  transfers between devices with their start and end apart: 6 -> 14, of which waited for: 6 -> 14; matrix products, arithmetic and copies ran while one was open for 4% -> 2% of each run, Pallas kernels for 0% -> 0%
where the time goes in v1:
time: 2260 us; the launch traced here: 2250 us
  waiting for transfers between devices  1740 us (77%)
  other arithmetic  339 us (15%)
  local copies, waits for them, and re-layouts  81.3 us (4%)
  matrix products  55.5 us (2%)
    ppermute x10, waiting for transfers between devices, fetch_columns(): lax.ppermute(gathered, 'row', [(dev, dev ^ hop) for dev in range(32)])  1420 us
    psum x2, waiting for transfers between devices, spread(): return lax.psum(kept, axis)  217 us
    another operation x29, other arithmetic, factor_step(): factor_local = jnp.linalg.cholesky(chosen)  158 us
    all_gather x2, waiting for transfers between devices, from_root(): lax.all_gather(shard, axis)  95.3 us
    another operation x5, other arithmetic, factor_step(): jax.scipy.linalg.solve_triangular(diag_block, source.reshape(local_rows *...  82.1 us
    add x9, other arithmetic, fetch_columns(): gathered + lax.ppermute(gathered, 'row', [(dev, dev ^ hop) for dev in ran...  78.1 us
  transfers between devices with their start and end apart: 14, of which 14 were waited for; matrix products, arithmetic and copies ran while one was open for 2% of the time, Pallas kernels for 0%

profile of v1, /device:TPU:1, one launch (start us, length us, event | category | flops | bytes accessed | tf_op | source)
XLA Modules:
  0.0 2250.0 jit_solution(12512748190144954325)
XLA Ops:
  6.5 20.5 copy.2
  27.1 1.3 convert_select_fusion.1
  28.8 1.5 fusion.12
  30.2 11.7 cholesky.286
  42.1 9.8 custom-call.27
  52.7 11.7 cholesky.305
  64.6 10.0 custom-call.28
  75.6 11.7 cholesky.326
  87.5 9.8 custom-call.29
  98.1 12.1 cholesky.343
  116.1 1.5 slice_bitcast_fusion.20
  117.6 107.4 %all-reduce.4.cloned.1.call-done = f32[512,512]{0,1:T(8,128)} async-done(((f32[512,512]{0,1:T(8,128)}), f32[512,512]{0,1:T(8,128)}) %all-reduce.4.cloned.1.call-update) | async-done | bytes 1048592 | tf_op jit(solution)/shard_map/psum | solution.py:12
  225.1 1.3 fusion.16
  226.4 9.1 while.10
  227.1 1.5 dynamic-slice.65
  229.4 1.5 dynamic-slice.65
  231.7 1.5 dynamic-slice.65
  233.9 1.5 dynamic-slice.65
  236.2 40.1 %custom-call.30 = f32[4,128,128]{1,2,0:T(8,128)S(1)} custom-call(f32[4,128,128]{2,1,0:T(8,128)} %copy-done.7), custom_call_target="InvertDiagBlocksLowerTriangular" | custom-call | tf_op jit(solution)/shard_map/jit(_solve_triangular)/triangular_solve | solution.py:69
  280.8 47.6 %all-gather.5.cloned.1.call-done = f32[2048,512]{0,1:T(8,128)} async-done(((f32[512,512]{0,1:T(8,128)}), f32[2048,512]{0,1:T(8,128)}) %all-gather.5.cloned.1.call-update) | async-done | bytes 4194320 | tf_op jit(solution)/shard_map/all_gather | solution.py:16
  331.7 12.8 collective-permute-done
  344.7 3.2 copy-done.1
  349.2 180.5 %collective-permute-done.1 = f32[1,8,512,512]{2,3,1,0:T(8,128)} collective-permute-done((f32[1,8,512,512]{2,3,1,0:T(8,128)S(1)}, f32[1,8,512,512]{2,3,1,0:T(8,128)}, u32[]{:S(2)}, u32[]{:S(2)}) %collective-permute-start.1) | collective-permute-done | bytes 8388640 | tf_op jit(solution)/shard_map/ppermute | solution.py:52
  529.7 11.1 add.112
  540.8 2.7 collective-permute-start.2
  543.5 179.9 %collective-permute-done.2 = f32[1,8,512,512]{2,3,1,0:T(8,128)} collective-permute-done((f32[1,8,512,512]{2,3,1,0:T(8,128)}, f32[1,8,512,512]{2,3,1,0:T(8,128)}, u32[]{:S(2)}, u32[]{:S(2)}) %collective-permute-start.2) | collective-permute-done | bytes 8388640 | tf_op jit(solution)/shard_map/ppermute | solution.py:52
  723.4 11.1 add.113
  735.7 179.0 %collective-permute-done.3 = f32[1,8,512,512]{2,3,1,0:T(8,128)} collective-permute-done((f32[1,8,512,512]{2,3,1,0:T(8,128)}, f32[1,8,512,512]{2,3,1,0:T(8,128)}, u32[]{:S(2)}, u32[]{:S(2)}) %collective-permute-start.3) | collective-permute-done | bytes 8388640 | tf_op jit(solution)/shard_map/ppermute | solution.py:52
  914.7 11.1 add.114
  925.8 3.0 collective-permute-start.4
  928.8 2.6 bitcast_dynamic-update-slice_fusion.6
  931.4 8.3 broadcast_select_fusion
  939.7 167.1 %collective-permute-done.4 = f32[1,8,512,512]{2,3,1,0:T(8,128)} collective-permute-done((f32[1,8,512,512]{2,3,1,0:T(8,128)}, f32[1,8,512,512]{2,3,1,0:T(8,128)}, u32[]{:S(2)}, u32[]{:S(2)}) %collective-permute-start.4) | collective-permute-done | bytes 8388640 | tf_op jit(solution)/shard_map/ppermute | solution.py:52
  1106.8 11.1 add.115
  1117.9 3.7 convert_select_fusion
  1123.3 11.7 cholesky.358
  1135.1 10.2 custom-call.31
  1148.0 11.7 cholesky.377
  1159.8 9.8 custom-call.32
  1170.1 1.5 convolution_subtract_fusion.9
  1171.6 11.7 cholesky.398
  1183.5 10.0 custom-call.33
  1195.1 11.7 cholesky.415
  1213.1 109.2 %all-reduce.6.cloned.1.call-done = f32[512,512]{0,1:T(8,128)} async-done(((f32[512,512]{0,1:T(8,128)}), f32[512,512]{0,1:T(8,128)}) %all-reduce.6.cloned.1.call-update) | async-done | bytes 1048592 | tf_op jit(solution)/shard_map/psum | solution.py:12
  1322.3 1.3 fusion.14
  1323.7 8.1 while.11
  1331.7 39.3 %custom-call.34 = f32[4,128,128]{1,2,0:T(8,128)S(1)} custom-call(f32[4,128,128]{2,1,0:T(8,128)S(1)} %get-tuple-element.94), custom_call_target="InvertDiagBlocksLowerTriangular" | custom-call | tf_op jit(solution)/shard_map/jit(_solve_triangular)/triangular_solve | solution.py:69
  1374.3 1.4 fusion.56
  1376.9 47.7 %all-gather.7.cloned.1.call-done = f32[2048,512]{1,0:T(8,128)} async-done(((f32[512,512]{1,0:T(8,128)}), f32[2048,512]{1,0:T(8,128)}) %all-gather.7.cloned.1.call-update) | async-done | bytes 4194320 | tf_op jit(solution)/shard_map/all_gather | solution.py:16
  1428.3 12.8 collective-permute-done.5
  1441.4 3.2 copy-done
  1445.8 180.5 %collective-permute-done.6 = f32[1,8,512,512]{2,3,1,0:T(8,128)} collective-permute-done((f32[1,8,512,512]{2,3,1,0:T(8,128)S(1)}, f32[1,8,512,512]{2,3,1,0:T(8,128)}, u32[]{:S(2)}, u32[]{:S(2)}) %collective-permute-start.6) | collective-permute-done | bytes 8388640 | tf_op jit(solution)/shard_map/ppermute | solution.py:52
  1626.4 11.1 add.117
  1637.4 2.9 collective-permute-start.7
  1640.4 179.9 %collective-permute-done.7 = f32[1,8,512,512]{2,3,1,0:T(8,128)} collective-permute-done((f32[1,8,512,512]{2,3,1,0:T(8,128)}, f32[1,8,512,512]{2,3,1,0:T(8,128)}, u32[]{:S(2)}, u32[]{:S(2)}) %collective-permute-start.7) | collective-permute-done | bytes 8388640 | tf_op jit(solution)/shard_map/ppermute | solution.py:52
  1820.2 11.1 add.118
  1832.6 179.0 %collective-permute-done.8 = f32[1,8,512,512]{2,3,1,0:T(8,128)} collective-permute-done((f32[1,8,512,512]{2,3,1,0:T(8,128)}, f32[1,8,512,512]{2,3,1,0:T(8,128)}, u32[]{:S(2)}, u32[]{:S(2)}) %collective-permute-start.8) | collective-permute-done | bytes 8388640 | tf_op jit(solution)/shard_map/ppermute | solution.py:52
  2011.6 11.1 add.119
  2022.6 2.9 collective-permute-start.9
  2027.7 17.1 bitcast_subtract_fusion
  2044.8 4.3 copy.100
  2050.4 153.2 %collective-permute-done.9 = f32[1,8,512,512]{2,3,1,0:T(8,128)} collective-permute-done((f32[1,8,512,512]{2,3,1,0:T(8,128)}, f32[1,8,512,512]{2,3,1,0:T(8,128)}, u32[]{:S(2)}, u32[]{:S(2)}) %collective-permute-start.9) | collective-permute-done | bytes 8388640 | tf_op jit(solution)/shard_map/ppermute | solution.py:52
  2203.5 19.0 subtract_bitcast_fusion
  2222.6 20.5 copy.35
  (161 shorter events, 53.7 us)
Async XLA Ops:
  6.5 218.5 %all-reduce.4.cloned.1.call-start = ((), (), s32[]{:S(2)}) async-start(), calls=%async_computation | async-start | bytes 2097152 | tf_op jit(solution)/shard_map/psum | solution.py:12
  116.1 212.4 %all-gather.5.cloned.1.call-start = ((), (), s32[]{:S(2)}) async-start(), calls=%async_computation.2 | async-start | bytes 5242880 | tf_op jit(solution)/shard_map/all_gather | solution.py:16
  235.5 0.7 copy-start.7
  280.8 1041.6 %all-reduce.6.cloned.1.call-start = ((), (), s32[]{:S(2)}) async-start(), calls=%async_computation.1 | async-start | bytes 2097152 | tf_op jit(solution)/shard_map/psum | solution.py:12
  328.4 2.2 copy-start.2
  330.7 13.7 collective-permute-start
  344.7 3.2 copy-start.1
  347.9 181.7 %collective-permute-start.1 = (f32[1,8,512,512]{2,3,1,0:T(8,128)S(1)}, f32[1,8,512,512]{2,3,1,0:T(8,128)}, u32[]{:S(2)}, u32[]{:S(2)}) collective-permute-start(f32[1,8,512,512]{2,3,1,0:T(8,128)S(1)} %fusion.11), channel_id=1, source_target_pairs={{0,8},{4,12},{8,0},{12,4},{16,24},{20,28},{24,16},{28,20},{32,40},... | collective-permute-start | bytes 25165832 | tf_op jit(solution)/shard_map/ppermute | solution.py:52
  540.8 182.6 %collective-permute-start.2 = (f32[1,8,512,512]{2,3,1,0:T(8,128)}, f32[1,8,512,512]{2,3,1,0:T(8,128)}, u32[]{:S(2)}, u32[]{:S(2)}) collective-permute-start(f32[1,8,512,512]{2,3,1,0:T(8,128)} %add.112), channel_id=1, source_target_pairs={{0,16},{4,20},{8,24},{12,28},{16,0},{20,4},{24,8},{28,12},{32,48},... | collective-permute-start | bytes 25165832 | tf_op jit(solution)/shard_map/ppermute | solution.py:52
  734.4 194.4 %copy-start.3 = (f32[512,512]{0,1:T(8,128)S(1)}, f32[512,512]{0,1:T(8,128)}, u32[]{:S(2)}) copy-start(f32[512,512]{0,1:T(8,128)} %all-reduce.4.cloned.1.call-done) | copy-start | bytes 3145732
  734.4 180.2 %collective-permute-start.3 = (f32[1,8,512,512]{2,3,1,0:T(8,128)}, f32[1,8,512,512]{2,3,1,0:T(8,128)}, u32[]{:S(2)}, u32[]{:S(2)}) collective-permute-start(f32[1,8,512,512]{2,3,1,0:T(8,128)} %add.113), channel_id=1, source_target_pairs={{0,32},{4,36},{8,40},{12,44},{16,48},{20,52},{24,56},{28,60},{32,0... | collective-permute-start | bytes 25165832 | tf_op jit(solution)/shard_map/ppermute | solution.py:52
  925.8 181.0 %collective-permute-start.4 = (f32[1,8,512,512]{2,3,1,0:T(8,128)}, f32[1,8,512,512]{2,3,1,0:T(8,128)}, u32[]{:S(2)}, u32[]{:S(2)}) collective-permute-start(f32[1,8,512,512]{2,3,1,0:T(8,128)} %add.114), channel_id=1, source_target_pairs={{0,64},{4,68},{8,72},{12,76},{16,80},{20,84},{24,88},{28,92},{32,9... | collective-permute-start | bytes 25165832 | tf_op jit(solution)/shard_map/ppermute | solution.py:52
  1122.2 1.1 copy-start.5
  1213.1 211.6 %all-gather.7.cloned.1.call-start = ((), (), s32[]{:S(2)}) async-start(), calls=%async_computation.3 | async-start | bytes 5242880 | tf_op jit(solution)/shard_map/all_gather | solution.py:16
  1371.1 1.8 copy-start.6
  1427.4 13.7 collective-permute-start.5
  1441.4 3.2 copy-start
  1444.6 181.7 %collective-permute-start.6 = (f32[1,8,512,512]{2,3,1,0:T(8,128)S(1)}, f32[1,8,512,512]{2,3,1,0:T(8,128)}, u32[]{:S(2)}, u32[]{:S(2)}) collective-permute-start(f32[1,8,512,512]{2,3,1,0:T(8,128)S(1)} %fusion.8), channel_id=1, source_target_pairs={{0,8},{4,12},{8,0},{12,4},{16,24},{20,28},{24,16},{28,20},{32,40},... | collective-permute-start | bytes 25165832 | tf_op jit(solution)/shard_map/ppermute | solution.py:52
  1637.4 182.8 %collective-permute-start.7 = (f32[1,8,512,512]{2,3,1,0:T(8,128)}, f32[1,8,512,512]{2,3,1,0:T(8,128)}, u32[]{:S(2)}, u32[]{:S(2)}) collective-permute-start(f32[1,8,512,512]{2,3,1,0:T(8,128)} %add.117), channel_id=1, source_target_pairs={{0,16},{4,20},{8,24},{12,28},{16,0},{20,4},{24,8},{28,12},{32,48},... | collective-permute-start | bytes 25165832 | tf_op jit(solution)/shard_map/ppermute | solution.py:52
  1831.3 180.2 %collective-permute-start.8 = (f32[1,8,512,512]{2,3,1,0:T(8,128)}, f32[1,8,512,512]{2,3,1,0:T(8,128)}, u32[]{:S(2)}, u32[]{:S(2)}) collective-permute-start(f32[1,8,512,512]{2,3,1,0:T(8,128)} %add.118), channel_id=1, source_target_pairs={{0,32},{4,36},{8,40},{12,44},{16,48},{20,52},{24,56},{28,60},{32,0... | collective-permute-start | bytes 25165832 | tf_op jit(solution)/shard_map/ppermute | solution.py:52
  2022.6 180.9 %collective-permute-start.9 = (f32[1,8,512,512]{2,3,1,0:T(8,128)}, f32[1,8,512,512]{2,3,1,0:T(8,128)}, u32[]{:S(2)}, u32[]{:S(2)}) collective-permute-start(f32[1,8,512,512]{2,3,1,0:T(8,128)} %add.119), channel_id=1, source_target_pairs={{0,64},{4,68},{8,72},{12,76},{16,80},{20,84},{24,88},{28,92},{32,9... | collective-permute-start | bytes 25165832 | tf_op jit(solution)/shard_map/ppermute | solution.py:52
  2044.7 158.8 %slice-start = ((s8[8388608]{0:T(1024)(128)(4,1)}), s8[4194304]{0:T(1024)(128)(4,1)S(1)}, s32[]{:S(2)}) async-start(s8[8388608]{0:T(1024)(128)(4,1)} %bitcast.167), calls=%async_computation.4 | async-start | bytes 8388608
  2044.8 4.3 copy-start.4
  2044.8 158.8 %slice-start.1 = ((s8[8388608]{0:T(1024)(128)(4,1)}), s8[4194304]{0:T(1024)(128)(4,1)S(1)}, s32[]{:S(2)}) async-start(s8[8388608]{0:T(1024)(128)(4,1)} %bitcast.167), calls=%async_computation.5 | async-start | bytes 8388608
Sparse Core Ops, SparseCore 0:
  116.2 108.8 all-reduce.3
  280.9 47.4 all-gather.4
  1213.2 109.0 all-reduce.5
  1377.1 47.5 all-gather.6
